TPU v7x, 256 devices: a whole 4x4x8 slice. The times are simulated.
256 devices in a mesh: ctx: 16 (over z_hi, x), tp: 4 (over y), dp: 4 (over z_lo, core).
Axes of the slice: x: 4, y: 4, z: 8 (z_hi: 4, z_lo: 2; z = z_hi * 2 + z_lo), core: 2. Of those that a mesh axis runs over, the one named last changes fastest.
Arguments:
- byte_embed: bfloat16 [65536, 1024], P(('dp', 'ctx', 'tp')), parts along dimension 0, may hold values from -6 to 6
- patch_start: int32 [65536], P(('dp', 'ctx', 'tp')), parts along dimension 0, may hold values from 0 to 1, as said below
- enc_gain: float32 [1024], replicated, may hold values from 0.1 to 1.9
- enc_qkv: bfloat16 [1024, 3072], replicated, may hold values from -4 to 4
- enc_out: bfloat16 [1024, 1024], replicated, may hold values from -0.1875 to 0.1875
- up_proj: bfloat16 [1024, 4096], P('ctx', 'tp'), may hold values from -0.1875 to 0.1875
- lat_gain: float32 [4096], replicated, may hold values from 0.1 to 1.9
- query_proj: bfloat16 [4096, 2048], P('ctx', 'tp'), may hold values from -4 to 4
- key_proj: bfloat16 [4096, 512], P('ctx', 'tp'), may hold values from -4 to 4
- value_matrix: bfloat16 [4096, 512], P('ctx', 'tp'), may hold values from -0.09375 to 0.09375
- out_proj: bfloat16 [2048, 4096], P('tp', 'ctx'), may hold values from -0.125 to 0.125
- down_proj: bfloat16 [4096, 1024], P('tp', 'ctx'), may hold values from -0.09375 to 0.09375
Outputs:
- byte_states: bfloat16 [65536, 1024], P(('dp', 'ctx', 'tp')), parts along dimension 0
There are 4 independent parts, one for each index of `dp`. A program takes and returns all parts, laid end to end along the dimension named above; an argument that names none is the same for every part. Nothing has to cross between parts.
Inputs may be any that keep to these rules, and one draw needn't show every extreme that they name: `patch_start`: byte 0 begins a patch; every patch spans 1 to 19 bytes; each aligned group of 1024 bytes holds at most 256 patch starts, and some group holds exactly 256.
All inputs are finite; a program needn't handle non-finite values.
Results may differ from a plain program's by a relative error of at most 0.015.
Values may be sent and summed in bfloat16 or wider, within the bound.
A program may use at most 128 MiB of HBM per device.

v0:
```python
import jax
import jax.numpy as jnp
from jax import lax
from jax.sharding import PartitionSpec as P

BH = 16
HB = 64
HEAD_SIZE = 128
WIN = 512
EPS = 1e-05


def shifted(block, axis, distance):
    devices = range(lax.axis_size(axis))
    route = [(i - distance, i) for i in devices if i - distance in devices]
    return lax.ppermute(block, axis, route)


def in_order(parts, dim):
    parts = jnp.moveaxis(parts, 0, dim)
    dims = parts.shape
    return parts.reshape(*dims[:dim], dims[dim] * dims[dim + 1], *dims[dim + 2 :])


def from_everyone(value, axis):
    copies = jnp.broadcast_to(value, (lax.axis_size(axis), *value.shape))
    return lax.all_to_all(copies, axis, split_axis=0, concat_axis=0, tiled=True)


def gathered_copies(value, axis, dim):
    return in_order(from_everyone(value, axis), dim)


def in_blocks(value, dim, peers):
    before, after = (value.shape[:dim], value.shape[dim + 1 :])
    return jnp.moveaxis(value.reshape(*before, peers, -1, *after), dim, 0)


def sum_at_owner(value, axis, dim):
    parts = in_blocks(value, dim, lax.axis_size(axis))
    arrived = lax.all_to_all(parts, axis, split_axis=0, concat_axis=0, tiled=True)
    return arrived.astype(jnp.float32).sum(axis=0)


def in_one_piece(arrays, axis, dim, along):
    columns = [a.reshape(*a.shape[:along], -1) for a in arrays]
    both = jnp.concatenate(columns, axis=along)
    result, at, gathered = (sum_at_owner(both, axis, dim), 0, [])
    for a, column in zip(arrays, columns):
        piece = result[..., at : at + column.shape[along]]
        gathered.append(piece.reshape(*piece.shape[:along], *a.shape[along:]))
        at += column.shape[along]
    return tuple(gathered)


def sent_together(arrays, axis, dim, along):
    ends, at = ([], 0)
    for a in arrays[:-1]:
        at += a.shape[along]
        ends.append(at)
    both = jnp.concatenate(arrays, axis=along)
    return tuple(jnp.split(lax.all_gather(both, axis, axis=dim, tiled=True), ends, axis=along))


def taken_together(value, axis):
    everything = from_everyone(value, axis)
    return jnp.sum(everything.astype(jnp.float32), axis=0)


def rms_scale(values, gain):
    floats = values.astype(jnp.float32)
    return floats * lax.rsqrt(jnp.mean(floats * floats, axis=-1, keepdims=True) + EPS) * gain


def window_attend(query, keys, values, first):
    n_query = query.shape[0]
    n_key = keys.shape[0]
    qh = query.reshape(n_query, BH, HB)
    kh = keys.reshape(n_key, BH, HB)
    vh = values.reshape(n_key, BH, HB)
    scores = jnp.einsum("qhd,khd->hqk", qh, kh, preferred_element_type=jnp.float32) / jnp.sqrt(
        jnp.float32(HB)
    )
    q_pos = first + jnp.arange(n_query, dtype=jnp.int32)
    k_pos = first - (n_key - n_query) + jnp.arange(n_key, dtype=jnp.int32)
    allowed = (
        (k_pos[None, :] <= q_pos[:, None])
        & (k_pos[None, :] > q_pos[:, None] - WIN)
        & (k_pos[None, :] >= 0)
    )
    scores = jnp.where(allowed[None], scores, jnp.float32(-1e30))
    peak = jnp.max(scores, axis=-1, keepdims=True)
    expo = jnp.where(allowed[None], jnp.exp(scores - peak), jnp.float32(0.0))
    total = jnp.sum(expo, axis=-1, keepdims=True)
    mixed = (
        jnp.einsum(
            "hqk,khd->hqd", expo.astype(jnp.bfloat16), vh, preferred_element_type=jnp.float32
        )
        / total
    )
    return jnp.transpose(mixed, (1, 0, 2)).reshape(n_query, BH * HB).astype(jnp.bfloat16)


def local(
    byte_embed,
    patch_start,
    enc_gain,
    enc_qkv,
    enc_out,
    up_proj,
    lat_gain,
    query_proj,
    key_proj,
    value_matrix,
    out_proj,
    down_proj,
):
    nbytes = byte_embed.shape[0]
    width = byte_embed.shape[1]
    n_tp = lax.axis_size("tp")
    n_ctx = lax.axis_size("ctx")
    device = lax.axis_index(("ctx", "tp"))
    group = device // n_tp
    slots = n_tp * nbytes // 4
    normed = rms_scale(byte_embed, enc_gain).astype(jnp.bfloat16)
    qkv = jnp.dot(normed, enc_qkv, preferred_element_type=jnp.float32).astype(jnp.bfloat16)
    query = qkv[:, :width]
    earlier = (qkv[:, width : 2 * width], qkv[:, 2 * width :])
    key_list = [earlier[0]]
    value_list = [earlier[1]]
    for step in range(2):
        earlier = shifted((earlier[0], earlier[1]), ("ctx", "tp"), 1)
        key_list.insert(0, earlier[0])
        value_list.insert(0, earlier[1])
    context = window_attend(
        query,
        jnp.concatenate(key_list, axis=0),
        jnp.concatenate(value_list, axis=0),
        device * nbytes,
    )
    hidden = (
        byte_embed.astype(jnp.float32)
        + jnp.dot(context, enc_out, preferred_element_type=jnp.float32)
    ).astype(jnp.bfloat16)
    local_count = jnp.sum(patch_start)
    all_counts = gathered_copies(local_count[None], ("ctx", "tp"), 0)
    before = jnp.cumsum(all_counts) - all_counts
    offset = before[device] - before[group * n_tp]
    group_counts = jnp.sum(all_counts.reshape(n_ctx, n_tp), axis=1)
    local_slot = jnp.cumsum(patch_start) - 1
    slot = offset + local_slot
    columns = jnp.arange(slots, dtype=jnp.int32)
    onehot = ((slot[:, None] == columns[None, :]) & (local_slot[:, None] >= 0)).astype(jnp.bfloat16)
    part_sum = jnp.dot(onehot.T, hidden, preferred_element_type=jnp.float32)
    part_count = jnp.sum(onehot.astype(jnp.float32), axis=0)
    leading = (local_slot < 0).astype(jnp.bfloat16)
    lead_sum = jnp.dot(leading[None, :], hidden, preferred_element_type=jnp.float32)
    lead_count = jnp.sum(leading.astype(jnp.float32))[None]
    recv_sum, recv_count = shifted((lead_sum, lead_count), ("ctx", "tp"), -1)
    last = offset + local_count - 1
    last_hot = (columns == last).astype(jnp.float32)
    part_sum = part_sum + last_hot[:, None] * recv_sum
    part_count = part_count + last_hot * recv_count
    sums, counts = in_one_piece(
        (part_sum.astype(jnp.bfloat16), part_count.astype(jnp.bfloat16)), "tp", 0, 1
    )
    share = (sums / jnp.maximum(counts, 1.0)[:, None]).astype(jnp.bfloat16)
    pooled = gathered_copies(share, "tp", 0)
    latent_part = jnp.dot(
        pooled,
        lax.all_gather(up_proj, "ctx", axis=0, tiled=True),
        preferred_element_type=jnp.float32,
    ).astype(jnp.bfloat16)
    latent = gathered_copies(latent_part, "tp", 1)
    lnorm = rms_scale(latent, lat_gain).astype(jnp.bfloat16)

    def proj_add(piece):
        return jnp.dot(lnorm, piece, preferred_element_type=jnp.float32)

    pieces = sent_together((query_proj, key_proj, value_matrix), "ctx", 0, 1)
    q_sum, k_sum, v_sum = tuple((proj_add(pieces[i]) for i in range(3)))
    q_local = q_sum.astype(jnp.bfloat16)
    k_local = k_sum.astype(jnp.bfloat16)
    v_local = v_sum.astype(jnp.bfloat16)
    heads_local = q_local.shape[1] // HEAD_SIZE
    kv_local = k_local.shape[1] // HEAD_SIZE
    share_count = heads_local // kv_local
    q_grouped = jnp.transpose(
        q_local.reshape(slots, kv_local, share_count, HEAD_SIZE), (1, 2, 0, 3)
    ).reshape(kv_local, share_count * slots, HEAD_SIZE)
    query_rows = group * slots + jnp.tile(jnp.arange(slots, dtype=jnp.int32), share_count)
    scale = 1.0 / jnp.sqrt(jnp.float32(HEAD_SIZE))
    peak = jnp.full((kv_local, share_count * slots), -1e30, jnp.float32)
    k_piece, v_piece = sent_together((k_local, v_local), "ctx", 0, 1)
    count = k_piece.shape[0]
    k_heads = jnp.transpose(k_piece.reshape(count, kv_local, HEAD_SIZE), (1, 0, 2))
    v_heads = jnp.transpose(v_piece.reshape(count, kv_local, HEAD_SIZE), (1, 0, 2))
    key_rows = jnp.arange(count, dtype=jnp.int32)
    used = key_rows % slots < group_counts[key_rows // slots]
    allowed = used[None, :] & (key_rows[None, :] <= query_rows[:, None])
    scores = (
        jnp.einsum("hqd,hkd->hqk", q_grouped, k_heads, preferred_element_type=jnp.float32) * scale
    )
    scores = jnp.where(allowed[None], scores, jnp.float32(-1e30))
    new_peak = jnp.maximum(peak, jnp.max(scores, axis=-1))
    expo = jnp.where(allowed[None], jnp.exp(scores - new_peak[..., None]), jnp.float32(0.0))
    total = jnp.sum(expo, axis=-1)
    accum = jnp.einsum(
        "hqk,hkd->hqd", expo.astype(jnp.bfloat16), v_heads, preferred_element_type=jnp.float32
    )
    peak, total, accum = (new_peak, total, accum)
    mixed = accum / total[..., None]
    attn = (
        jnp.transpose(mixed.reshape(kv_local, share_count, slots, HEAD_SIZE), (2, 0, 1, 3))
        .reshape(slots, heads_local * HEAD_SIZE)
        .astype(jnp.bfloat16)
    )
    partial_value = jnp.dot(
        attn,
        lax.all_gather(out_proj, "ctx", axis=1, tiled=True),
        preferred_element_type=jnp.float32,
    )
    attn_part = sum_at_owner(partial_value.astype(jnp.bfloat16), "tp", 1)
    latent_out = (latent_part.astype(jnp.float32) + attn_part).astype(jnp.bfloat16)
    down_part = jnp.dot(
        latent_out,
        lax.all_gather(down_proj, "ctx", axis=1, tiled=True),
        preferred_element_type=jnp.float32,
    )
    patch_out = (
        taken_together(down_part.astype(jnp.bfloat16), "tp")
        .astype(jnp.float32)
        .astype(jnp.bfloat16)
    )
    trailing = lax.dynamic_slice_in_dim(patch_out, last, 1, 0)
    carried = shifted(trailing, ("ctx", "tp"), 1)
    spread = jnp.dot(onehot, patch_out, preferred_element_type=jnp.float32) + leading.astype(
        jnp.float32
    )[:, None] * carried.astype(jnp.float32)
    return (hidden.astype(jnp.float32) + spread).astype(jnp.bfloat16)


def solution(mesh):
    placed = (
        P(("dp", "ctx", "tp"), None),
        P(("dp", "ctx", "tp")),
        P(),
        P(),
        P(),
        P("ctx", "tp"),
        P(),
        P("ctx", "tp"),
        P("ctx", "tp"),
        P("ctx", "tp"),
        P("tp", "ctx"),
        P("tp", "ctx"),
    )
    return jax.shard_map(
        local, mesh=mesh, in_specs=placed, out_specs=P(("dp", "ctx", "tp"), None), check_vma=False
    )
```

profile of v0, /device:TPU:64, one launch (start us, length us, event | category | flops | bytes accessed | tf_op | source)
XLA Modules:
  0.0 502.0 jit_solution(70620909785672022)
XLA Ops:
  7.3 1.8 pad_maximum_fusion.3
  9.1 1.4 reduce_sum.106
  10.5 1.2 broadcast_in_dim.40
  11.8 13.8 %all-to-all-start = ((s32[64,1,1]{2,1,0:T(1,128)}), s32[64,1,1]{2,1,0:T(1,128)S(1)}, u32[]{:S(2)}, u32[]{:S(2)}) async-start(s32[64,1,1]{2,1,0:T(1,128)} %broadcast_in_dim.40), calls=%async_computation | async-start | bytes 65536 | tf_op jit(solution)/shard_map/all_to_all | solution.py:27
  26.8 4.9 convolution_convert_fusion.1
  32.6 3.4 collective-permute-start
  36.0 3.4 collective-permute-start.2
  40.6 7.6 %collective-permute-start.5 = (f32[1]{0:T(128)}, f32[1]{0:T(128)}, u32[]{:S(2)}, u32[]{:S(2)}) collective-permute-start(f32[1]{0:T(128)} %bitcast.15), channel_id=1, source_target_pairs={{4,0},{8,4},{12,8},{16,12},{20,16},{24,20},{28,24},{32,28},{36,32}... | collective-permute-start | bytes 20 | tf_op jit(solution)/shard_map/ppermute | solution.py:16
  53.0 2.2 collective-permute-done
  55.2 1.9 collective-permute-start.1
  57.2 22.2 %collective-permute-done.2 = bf16[256,1024]{1,0:T(8,128)(2,1)} collective-permute-done((bf16[256,1024]{1,0:T(8,128)(2,1)S(1)}, bf16[256,1024]{1,0:T(8,128)(2,1)}, u32[]{:S(2)}, u32[]{:S(2)}) %collective-permute-start.2) | collective-permute-done | bytes 524320 | tf_op jit(solution)/shard_map/ppermute | solution.py:16
  79.4 1.9 collective-permute-start.3
  82.8 7.7 %collective-permute-done.1 = bf16[256,1024]{1,0:T(8,128)(2,1)S(1)} collective-permute-done((bf16[256,1024]{1,0:T(8,128)(2,1)}, bf16[256,1024]{1,0:T(8,128)(2,1)S(1)}, u32[]{:S(2)}, u32[]{:S(2)}) %collective-permute-start.1) | collective-permute-done | bytes 524320 | tf_op jit(solution)/shard_map/ppermute | solution.py:16
  90.5 2.5 pad_maximum_fusion
  93.0 2.6 copy.46
  95.6 5.0 collective-permute-done.3
  100.6 2.5 pad_maximum_fusion.1
  103.1 2.6 copy.47
  105.7 8.4 %fusion.75 = (f32[16,256]{1,0:T(8,128)S(1)}, bf16[16,256,768]{2,1,0:T(8,128)(2,1)}) fusion(pred[256,768]{1,0:T(8,128)(4,1)S(1)} %and_and_fusion, bf16[256,16,64]{0,2,1:T(8,128)(2,1)S(1)} %bitcast.98, bf16[768,16,64]{0,2,1:T(8,128)(2,1)} %bitcast.94), kind=kOutput, calls=%fused_computation.127 | convolution fusion | flops 421528320 | bytes 8601600 | tf_op jit(solution)/shard_map/sub | solution.py:93
  114.1 5.3 %fusion.33 = bf16[256,16,64]{0,2,1:T(8,128)(2,1)S(1)} fusion(bf16[768,16,64]{0,2,1:T(8,128)(2,1)} %bitcast.95, bf16[16,256,768]{2,1,0:T(8,128)(2,1)} %get-tuple-element.30, f32[256,16]{0,1:T(8,128)S(1)} %bitcast.111), kind=kOutput, calls=%fused_computation.41 | convolution fusion | flops 403177472 | bytes 8404992 | tf_op jit(solution)/shard_map/hqk,khd->hqd/dot_general | solution.py:96
  120.3 1.9 collective-permute-start.4
  122.4 3.4 collective-permute-done.4
  126.3 10.8 %all_to_all.31 = bf16[4,64,1025]{2,1,0:T(8,128)(2,1)S(1)} all-to-all(bf16[4,64,1025]{2,1,0:T(8,128)(2,1)S(1)} %pad_maximum_fusion.2), channel_id=1, replica_groups=mesh['ctx'=16,'tp'=4,'dp'=4] {'tp'}, dimensions={0} | all-to-all | bytes 1049600 | tf_op jit(solution)/shard_map/all_to_all | solution.py:41
  137.5 10.5 %all_to_all.32 = bf16[4,64,1024]{2,1,0:T(8,128)(2,1)S(1)} all-to-all(bf16[4,64,1024]{2,1,0:T(8,128)(2,1)S(1)} %broadcast_in_dim.42), channel_id=1, replica_groups=mesh['ctx'=16,'tp'=4,'dp'=4] {'tp'}, dimensions={0} | all-to-all | bytes 1048576 | tf_op jit(solution)/shard_map/all_to_all | solution.py:27
  148.0 2.3 convolution_convert_fusion.3
  150.7 25.1 %all_to_all.33 = bf16[4,256,1024]{1,2,0:T(8,128)(2,1)S(1)} all-to-all(bf16[4,256,1024]{1,2,0:T(8,128)(2,1)S(1)} %broadcast_in_dim.43), channel_id=1, replica_groups=mesh['ctx'=16,'tp'=4,'dp'=4] {'tp'}, dimensions={0} | all-to-all | bytes 4194304 | tf_op jit(solution)/shard_map/all_to_all | solution.py:27
  176.3 1.7 fusion.14
  178.0 46.4 %all-gather.8.cloned.1.call-done = bf16[4096,768]{1,0:T(8,128)(2,1)} async-done(((bf16[256,768]{1,0:T(8,128)(2,1)}), bf16[4096,768]{1,0:T(8,128)(2,1)}) %all-gather.8.cloned.1.call-update) | async-done | bytes 6291472 | tf_op jit(solution)/shard_map/all_gather | solution.py:62
  224.5 2.4 convolution_convert_fusion.4
  226.9 2.4 convolution_convert_fusion.5
  232.7 4.3 compare_select_fusion.1
  237.0 5.6 %fusion.63 = pred[4096]{0:T(1024)(128)(4,1)S(1)} fusion(pred[4096]{0:T(1024)(128)(4,1)S(1)} %compare_reduce_fusion, pred[4096]{0:T(1024)(128)(4,1)S(1)} %compare_reduce_fusion.1, pred[4096]{0:T(1024)(128)(4,1)S(1)} %compare_reduce_fusion.2, pred[4096]{0:T(1024)(128)(4,1)S(1)} %compare_reduce_fusion.3, pred[4096]{0:T(1024)(128)(4,1)S(1)} %compare_reduce_fusion.4, ...), kind=kLoop, calls=%fused_computation.96 | loop fusion | flops 65536 | bytes 57380 | tf_op jit(solution)/shard_map/lt | solution.py:199
  242.6 3.4 fusion.27
  246.2 60.9 %all-gather.10.cloned.1.call-done = bf16[4096,256]{0,1:T(8,128)(2,1)} async-done(((bf16[256,256]{0,1:T(8,128)(2,1)}), bf16[4096,256]{0,1:T(8,128)(2,1)}) %all-gather.10.cloned.1.call-update) | async-done | bytes 2097168 | tf_op jit(solution)/shard_map/all_gather | solution.py:62
  307.1 6.7 %fusion.2 = (f32[1024]{0:T(1024)S(1)}, f32[1024,4096]{1,0:T(8,128)S(1)}) fusion(s32[1024]{0:T(1024)S(1)} %bitcast.105, pred[4096]{0:T(1024)(128)(4,1)S(1)} %fusion.63, bf16[1024,128]{1,0:T(8,128)(2,1)S(1)} %bitcast.102, bf16[4096,256]{0,1:T(8,128)(2,1)} %all-gather.10.cloned.1.call-done), kind=kOutput, calls=%fused_computation.5 | convolution fusion | flops 1094712320 | bytes 18100224 | tf_op jit(solution)/shard_map/hqd,hkd->hqk/dot_general | solution.py:202
  313.8 7.7 %fusion.70 = f32[1024]{0:T(1024)S(1)} fusion(f32[1024]{0:T(1024)S(1)} %broadcast_maximum_fusion, f32[1024,4096]{1,0:T(8,128)S(1)} %get-tuple-element.32, s32[1024]{0:T(1024)S(1)} %bitcast.106, pred[4096]{0:T(1024)(128)(4,1)S(1)} %fusion.63), kind=kLoop, calls=%fused_computation.123 | loop fusion | flops 29359104 | bytes 16793600 | tf_op jit(solution)/shard_map/reduce_sum | solution.py:207
  321.5 6.0 %fusion.24 = bf16[1024,128]{1,0:T(8,128)(2,1)S(1)} fusion(bf16[4096,256]{0,1:T(8,128)(2,1)S(1)} %copy-done.7, f32[1024]{0:T(1024)S(1)} %fusion.70, f32[1024,4096]{1,0:T(8,128)S(1)} %get-tuple-element.32, f32[1024]{0:T(1024)S(1)} %broadcast_maximum_fusion, s32[1024]{0:T(1024)S(1)} %bitcast.107, pred[4096]{0:T(1024)(128)(4,1)S(1)} %fusion.63), kind=kOutput, calls=%fused_computation.37 | convolution fusion | flops 1103364096 | bytes 18104320 | tf_op jit(solution)/shard_map/hqk,hkd->hqd/dot_general | solution.py:208
  327.6 61.0 %all-gather.12.cloned.1.call-done = bf16[512,4096]{1,0:T(8,128)(2,1)} async-done(((bf16[512,256]{1,0:T(8,128)(2,1)}), bf16[512,4096]{1,0:T(8,128)(2,1)}) %all-gather.12.cloned.1.call-update) | async-done | bytes 4194320 | tf_op jit(solution)/shard_map/all_gather | solution.py:220
  388.6 3.5 convolution_convert_fusion
  392.2 27.1 %all_to_all.34 = bf16[4,256,1024]{2,1,0:T(8,128)(2,1)S(1)} all-to-all(bf16[4,256,1024]{2,1,0:T(8,128)(2,1)S(1)} %bitcast.93), channel_id=1, replica_groups=mesh['ctx'=16,'tp'=4,'dp'=4] {'tp'}, dimensions={0} | all-to-all | bytes 4194304 | tf_op jit(solution)/shard_map/all_to_all | solution.py:41
  419.8 28.2 %all-gather.14.cloned.1.call-done = bf16[1024,1024]{0,1:T(8,128)(2,1)} async-done(((bf16[1024,64]{0,1:T(8,128)(2,1)}), bf16[1024,1024]{0,1:T(8,128)(2,1)}) %all-gather.14.cloned.1.call-update) | async-done | bytes 2097168 | tf_op jit(solution)/shard_map/all_gather | solution.py:227
  448.0 2.3 convolution_convert_fusion.2
  450.4 1.6 broadcast_in_dim.82
  452.0 4.4 all-to-all-start.5
  456.4 25.2 %all-to-all-done.5 = bf16[4,256,1024]{2,1,0:T(8,128)(2,1)} async-done(((bf16[4,256,1024]{2,1,0:T(8,128)(2,1)}), bf16[4,256,1024]{2,1,0:T(8,128)(2,1)}, u32[]{:S(2)}, u32[]{:S(2)}) %all-to-all-start.5) | async-done | bytes 2097184 | tf_op jit(solution)/shard_map/all_to_all | solution.py:27
  481.6 2.0 reduce_sum.115
  483.7 2.5 collective-permute-start.6
  486.2 8.1 %collective-permute-done.6 = bf16[1,1024]{1,0:T(2,128)(2,1)S(1)} collective-permute-done((bf16[1,1024]{1,0:T(2,128)(2,1)S(1)}, bf16[1,1024]{1,0:T(2,128)(2,1)S(1)}, u32[]{:S(2)}, u32[]{:S(2)}) %collective-permute-start.6) | collective-permute-done | bytes 2080 | tf_op jit(solution)/shard_map/ppermute | solution.py:16
  (92 shorter events, 16.6 us)
Async XLA Ops:
  6.5 112.9 %copy-start = (bf16[1024,1024]{1,0:T(8,128)(2,1)S(1)}, bf16[1024,1024]{1,0:T(8,128)(2,1)}, u32[]{:S(2)}) copy-start(bf16[1024,1024]{1,0:T(8,128)(2,1)} %param.16) | copy-start | bytes 6291460
  6.5 141.5 %all-gather.6.cloned.1.call-start = ((), (), s32[]{:S(2)}) async-start(), calls=%async_computation.6 | async-start | bytes 2228224 | tf_op jit(solution)/shard_map/all_gather | solution.py:171
  7.3 217.2 %all-gather.8.cloned.1.call-start = ((), (), s32[]{:S(2)}) async-start(), calls=%async_computation.7 | async-start | bytes 6684672 | tf_op jit(solution)/shard_map/all_gather | solution.py:62
  11.8 37.8 %all-to-all-start = ((s32[64,1,1]{2,1,0:T(1,128)}), s32[64,1,1]{2,1,0:T(1,128)S(1)}, u32[]{:S(2)}, u32[]{:S(2)}) async-start(s32[64,1,1]{2,1,0:T(1,128)} %broadcast_in_dim.40), calls=%async_computation | async-start | bytes 65536 | tf_op jit(solution)/shard_map/all_to_all | solution.py:27
  25.5 281.5 %all-gather.10.cloned.1.call-start = ((), (), s32[]{:S(2)}) async-start(), calls=%async_computation.8 | async-start | bytes 2228224 | tf_op jit(solution)/shard_map/all_gather | solution.py:62
  26.8 12.5 %copy-start.6 = (s32[256]{0:T(256)S(1)}, s32[256]{0:T(256)}, u32[]{:S(2)}) copy-start(s32[256]{0:T(256)} %param.13) | copy-start | bytes 3076
  32.6 22.6 %collective-permute-start = (bf16[256,1024]{1,0:T(8,128)(2,1)}, bf16[256,1024]{1,0:T(8,128)(2,1)}, u32[]{:S(2)}, u32[]{:S(2)}) collective-permute-start(bf16[256,1024]{1,0:T(8,128)(2,1)} %get-tuple-element.8), channel_id=1, source_target_pairs={{0,4},{4,8},{8,12},{12,16},{16,20},{20,24},{24,28},{28,32},{32,36}... | collective-permute-start | bytes 1572872 | tf_op jit(solution)/shard_map/ppermute | solution.py:16
  36.0 43.4 %collective-permute-start.2 = (bf16[256,1024]{1,0:T(8,128)(2,1)S(1)}, bf16[256,1024]{1,0:T(8,128)(2,1)}, u32[]{:S(2)}, u32[]{:S(2)}) collective-permute-start(bf16[256,1024]{1,0:T(8,128)(2,1)S(1)} %get-tuple-element.9), channel_id=1, source_target_pairs={{0,4},{4,8},{8,12},{12,16},{16,20},{20,24},{24,28},{28,32},{32,36}... | collective-permute-start | bytes 1572872 | tf_op jit(solution)/shard_map/ppermute | solution.py:16
  40.6 41.6 %collective-permute-start.5 = (f32[1]{0:T(128)}, f32[1]{0:T(128)}, u32[]{:S(2)}, u32[]{:S(2)}) collective-permute-start(f32[1]{0:T(128)} %bitcast.15), channel_id=1, source_target_pairs={{4,0},{8,4},{12,8},{16,12},{20,16},{24,20},{28,24},{32,28},{36,32}... | collective-permute-start | bytes 20 | tf_op jit(solution)/shard_map/ppermute | solution.py:16
  55.2 35.3 %collective-permute-start.1 = (bf16[256,1024]{1,0:T(8,128)(2,1)}, bf16[256,1024]{1,0:T(8,128)(2,1)S(1)}, u32[]{:S(2)}, u32[]{:S(2)}) collective-permute-start(bf16[256,1024]{1,0:T(8,128)(2,1)} %collective-permute-done), channel_id=1, source_target_pairs={{0,4},{4,8},{8,12},{12,16},{16,20},{20,24},{24,28},{28,32},{32,36}... | collective-permute-start | bytes 1572872 | tf_op jit(solution)/shard_map/ppermute | solution.py:16
  79.4 21.2 %collective-permute-start.3 = (bf16[256,1024]{1,0:T(8,128)(2,1)}, bf16[256,1024]{1,0:T(8,128)(2,1)}, u32[]{:S(2)}, u32[]{:S(2)}) collective-permute-start(bf16[256,1024]{1,0:T(8,128)(2,1)} %collective-permute-done.2), channel_id=1, source_target_pairs={{0,4},{4,8},{8,12},{12,16},{16,20},{20,24},{24,28},{28,32},{32,36}... | collective-permute-start | bytes 1572872 | tf_op jit(solution)/shard_map/ppermute | solution.py:16
  93.0 12.7 %copy-start.4 = (bf16[256,1024]{0,1:T(8,128)(2,1)S(1)}, bf16[256,1024]{0,1:T(8,128)(2,1)}, u32[]{:S(2)}) copy-start(bf16[256,1024]{0,1:T(8,128)(2,1)} %copy.45) | copy-start | bytes 1572868
  114.1 5.3 %copy-start.3 = (bf16[256,1024]{1,0:T(8,128)(2,1)S(1)}, bf16[256,1024]{1,0:T(8,128)(2,1)}, u32[]{:S(2)}) copy-start(bf16[256,1024]{1,0:T(8,128)(2,1)} %param.12) | copy-start | bytes 1572868
  120.3 5.5 %collective-permute-start.4 = (f32[1,1024]{1,0:T(1,128)S(1)}, f32[1,1024]{1,0:T(1,128)S(1)}, u32[]{:S(2)}, u32[]{:S(2)}) collective-permute-start(f32[1,1024]{1,0:T(1,128)S(1)} %fusion.76), channel_id=1, source_target_pairs={{4,0},{8,4},{12,8},{16,12},{20,16},{24,20},{28,24},{32,28},{36,32}... | collective-permute-start | bytes 12296 | tf_op jit(solution)/shard_map/ppermute | solution.py:16
  150.5 25.8 %copy-start.5 = (f32[4096]{0:T(1024)S(1)}, f32[4096]{0:T(1024)}, u32[]{:S(2)}) copy-start(f32[4096]{0:T(1024)} %param.18) | copy-start | bytes 49156
  178.0 64.6 %copy-start.2 = (bf16[256,4096]{0,1:T(8,128)(2,1)S(1)}, bf16[256,4096]{0,1:T(8,128)(2,1)}, u32[]{:S(2)}) copy-start(bf16[256,4096]{0,1:T(8,128)(2,1)} %fusion.14) | copy-start | bytes 6291460
  230.0 158.6 %all-gather.12.cloned.1.call-start = ((), (), s32[]{:S(2)}) async-start(), calls=%async_computation.9 | async-start | bytes 4456448 | tf_op jit(solution)/shard_map/all_gather | solution.py:220
  230.6 217.4 %all-gather.14.cloned.1.call-start = ((), (), s32[]{:S(2)}) async-start(), calls=%async_computation.10 | async-start | bytes 2228224 | tf_op jit(solution)/shard_map/all_gather | solution.py:227
  313.8 7.7 %copy-start.7 = (bf16[4096,256]{0,1:T(8,128)(2,1)S(1)}, bf16[4096,256]{0,1:T(8,128)(2,1)}, u32[]{:S(2)}) copy-start(bf16[4096,256]{0,1:T(8,128)(2,1)} %all-gather.10.cloned.1.call-done) | copy-start | bytes 6291460
  450.4 45.1 %copy-start.1 = (bf16[1024,1024]{1,0:T(8,128)(2,1)S(1)}, bf16[1024,1024]{1,0:T(8,128)(2,1)}, u32[]{:S(2)}) copy-start(bf16[1024,1024]{1,0:T(8,128)(2,1)} %param.16) | copy-start | bytes 6291460
  452.0 29.7 %all-to-all-start.5 = ((bf16[4,256,1024]{2,1,0:T(8,128)(2,1)}), bf16[4,256,1024]{2,1,0:T(8,128)(2,1)}, u32[]{:S(2)}, u32[]{:S(2)}) async-start(bf16[4,256,1024]{2,1,0:T(8,128)(2,1)} %broadcast_in_dim.82), calls=%async_computation.5 | async-start | bytes 4194304 | tf_op jit(solution)/shard_map/all_to_all | solution.py:27
  483.7 10.6 %collective-permute-start.6 = (bf16[1,1024]{1,0:T(2,128)(2,1)S(1)}, bf16[1,1024]{1,0:T(2,128)(2,1)S(1)}, u32[]{:S(2)}, u32[]{:S(2)}) collective-permute-start(bf16[1,1024]{1,0:T(2,128)(2,1)S(1)} %constant_dynamic-slice_fusion), channel_id=1, source_target_pairs={{0,4},{4,8},{8,12},{12,16},{16,20},{20,24},{24,28},{28,32},{32,36}... | collective-permute-start | bytes 6152 | tf_op jit(solution)/shard_map/ppermute | solution.py:16
Sparse Core Ops, SparseCore 0:
  9.8 61.1 all-gather.5
  73.4 151.0 all-gather.7
  230.1 76.9 all-gather.9
  309.3 79.2 all-gather.11
  390.9 57.1 all-gather.13
where the time goes:
time: 503 us; the launch traced here: 502 us
  waiting for transfers between devices  272 us (54%)
  blocking collectives  73.5 us (15%)
  matrix products  50.1 us (10%)
  starting transfers between devices  40.9 us (8%)
  other arithmetic  36.8 us (7%)
  between operations  15.6 us (3%)
  local copies, waits for them, and re-layouts  12.8 us (3%)
    all_gather x2, waiting for transfers between devices, sent_together(): lax.all_gather(both, axis, axis=dim, tiled=True)  107 us
    all_gather x1, waiting for transfers between devices, local(): lax.all_gather(out_proj, 'ctx', axis=1, tiled=True)  61 us
    ppermute x7, waiting for transfers between devices, shifted(): return lax.ppermute(block, axis, route)  48.8 us
    all_to_all x2, blocking collectives, sum_at_owner(): lax.all_to_all(parts, axis, split_axis=0, concat_axis=0, tiled=True)  38 us
    all_to_all x2, blocking collectives, from_everyone(): return lax.all_to_all(copies, axis, split_axis=0, concat_axis=0, tiled=True)  35.6 us
    all_gather x1, waiting for transfers between devices, local(): lax.all_gather(down_proj, 'ctx', axis=1, tiled=True)  28.2 us
    all_to_all x2, waiting for transfers between devices, from_everyone(): return lax.all_to_all(copies, axis, split_axis=0, concat_axis=0, tiled=True)  25.2 us
    ppermute x7, starting transfers between devices, shifted(): return lax.ppermute(block, axis, route)  22.5 us
  transfers between devices with their start and end apart: 14, of which 11 were waited for; matrix products, arithmetic and copies ran while one was open for 17% of the time, Pallas kernels for 0%

commit v1 on v0

--- a/solution.py
+++ b/solution.py
@@ -222,11 +222,16 @@
     )
     attn_part = sum_at_owner(partial_value.astype(jnp.bfloat16), "tp", 1)
     latent_out = (latent_part.astype(jnp.float32) + attn_part).astype(jnp.bfloat16)
-    down_part = jnp.dot(
-        latent_out,
-        lax.all_gather(down_proj, "ctx", axis=1, tiled=True),
-        preferred_element_type=jnp.float32,
-    )
+    serve_rates = lambda body: jnp.concatenate(
+        lax.all_to_all(
+            jnp.stack([body for _ in range(lax.axis_size("ctx"))]),
+            axis_name="ctx",
+            split_axis=0,
+            concat_axis=0,
+        ),
+        axis=1,
+    )
+    down_part = jnp.dot(latent_out, serve_rates(down_proj), preferred_element_type=jnp.float32)
     patch_out = (
         taken_together(down_part.astype(jnp.bfloat16), "tp")
         .astype(jnp.float32)

time: 503 us -> 535 us (1.064)
  waiting for transfers between devices: 272 us -> 291 us
  starting transfers between devices: 40.9 us -> 49.9 us
    all_to_all x0 -> x1, waiting for transfers between devices: none -> 46.2 us  [local(): lax.all_to_all(jnp.stack([body for _ in range(lax.axis_size('ctx'))]), ax...]
    all_gather x1 -> x0, waiting for transfers between devices: 28.2 us -> none  [local(): lax.all_gather(down_proj, 'ctx', axis=1, tiled=True)]
    all_to_all x0 -> x1, starting transfers between devices: none -> 9.03 us  [local(): lax.all_to_all(jnp.stack([body for _ in range(lax.axis_size('ctx'))]), ax...]
  transfers between devices with their start and end apart: 14 -> 14, of which waited for: 11 -> 11; matrix products, arithmetic and copies ran while one was open for 17% -> 16% of each run, Pallas kernels for 0% -> 0%
where the time goes in v1:
time: 535 us; the launch traced here: 534 us
  waiting for transfers between devices  291 us (54%)
  blocking collectives  74.3 us (14%)
  starting transfers between devices  49.9 us (9%)
  matrix products  49.6 us (9%)
  other arithmetic  38.5 us (7%)
  between operations  15.6 us (3%)
  local copies, waits for them, and re-layouts  15 us (3%)
    all_gather x2, waiting for transfers between devices, sent_together(): lax.all_gather(both, axis, axis=dim, tiled=True)  108 us
    all_gather x1, waiting for transfers between devices, local(): lax.all_gather(out_proj, 'ctx', axis=1, tiled=True)  61 us
    ppermute x7, waiting for transfers between devices, shifted(): return lax.ppermute(block, axis, route)  48.8 us
    all_to_all x1, waiting for transfers between devices, local(): lax.all_to_all(jnp.stack([body for _ in range(lax.axis_size('ctx'))]), ax...  46.2 us
    all_to_all x2, blocking collectives, sum_at_owner(): lax.all_to_all(parts, axis, split_axis=0, concat_axis=0, tiled=True)  38.7 us
    all_to_all x2, blocking collectives, from_everyone(): return lax.all_to_all(copies, axis, split_axis=0, concat_axis=0, tiled=True)  35.6 us
    all_to_all x2, waiting for transfers between devices, from_everyone(): return lax.all_to_all(copies, axis, split_axis=0, concat_axis=0, tiled=True)  25.8 us
    ppermute x7, starting transfers between devices, shifted(): return lax.ppermute(block, axis, route)  22.5 us
  transfers between devices with their start and end apart: 14, of which 11 were waited for; matrix products, arithmetic and copies ran while one was open for 16% of the time, Pallas kernels for 0%

profile of v1, /device:TPU:64, one launch (start us, length us, event | category | flops | bytes accessed | tf_op | source)
XLA Modules:
  0.0 533.8 jit_solution(14810680833382454426)
XLA Ops:
  7.3 1.8 pad_maximum_fusion.3
  11.8 13.8 %all-to-all-start = ((s32[64,1,1]{2,1,0:T(1,128)}), s32[64,1,1]{2,1,0:T(1,128)S(1)}, u32[]{:S(2)}, u32[]{:S(2)}) async-start(s32[64,1,1]{2,1,0:T(1,128)} %broadcast_in_dim.40), calls=%async_computation | async-start | bytes 65536 | tf_op jit(solution)/shard_map/all_to_all | solution.py:27
  26.8 4.9 convolution_convert_fusion.1
  32.6 3.4 collective-permute-start
  36.0 3.4 collective-permute-start.2
  40.6 7.6 %collective-permute-start.5 = (f32[1]{0:T(128)}, f32[1]{0:T(128)}, u32[]{:S(2)}, u32[]{:S(2)}) collective-permute-start(f32[1]{0:T(128)} %bitcast.15), channel_id=1, source_target_pairs={{4,0},{8,4},{12,8},{16,12},{20,16},{24,20},{28,24},{32,28},{36,32}... | collective-permute-start | bytes 20 | tf_op jit(solution)/shard_map/ppermute | solution.py:16
  53.0 2.2 collective-permute-done
  55.2 1.9 collective-permute-start.1
  57.2 22.2 %collective-permute-done.2 = bf16[256,1024]{1,0:T(8,128)(2,1)} collective-permute-done((bf16[256,1024]{1,0:T(8,128)(2,1)S(1)}, bf16[256,1024]{1,0:T(8,128)(2,1)}, u32[]{:S(2)}, u32[]{:S(2)}) %collective-permute-start.2) | collective-permute-done | bytes 524320 | tf_op jit(solution)/shard_map/ppermute | solution.py:16
  79.4 1.9 collective-permute-start.3
  82.8 7.7 %collective-permute-done.1 = bf16[256,1024]{1,0:T(8,128)(2,1)S(1)} collective-permute-done((bf16[256,1024]{1,0:T(8,128)(2,1)}, bf16[256,1024]{1,0:T(8,128)(2,1)S(1)}, u32[]{:S(2)}, u32[]{:S(2)}) %collective-permute-start.1) | collective-permute-done | bytes 524320 | tf_op jit(solution)/shard_map/ppermute | solution.py:16
  90.5 2.5 pad_maximum_fusion
  93.0 2.6 copy.47
  95.6 5.0 collective-permute-done.3
  100.6 2.5 pad_maximum_fusion.1
  103.1 2.6 copy.48
  105.7 8.4 %fusion.75 = (f32[16,256]{1,0:T(8,128)S(1)}, bf16[16,256,768]{2,1,0:T(8,128)(2,1)}) fusion(pred[256,768]{1,0:T(8,128)(4,1)S(1)} %and_and_fusion, bf16[256,16,64]{0,2,1:T(8,128)(2,1)S(1)} %bitcast.102, bf16[768,16,64]{0,2,1:T(8,128)(2,1)} %bitcast.98), kind=kOutput, calls=%fused_computation.127 | convolution fusion | flops 421528320 | bytes 8601600 | tf_op jit(solution)/shard_map/sub | solution.py:93
  114.1 5.3 fusion.33
  120.3 1.9 collective-permute-start.4
  122.4 3.4 collective-permute-done.4
  126.4 10.8 %all_to_all.36 = bf16[4,64,1025]{2,1,0:T(8,128)(2,1)S(1)} all-to-all(bf16[4,64,1025]{2,1,0:T(8,128)(2,1)S(1)} %pad_maximum_fusion.2), channel_id=1, replica_groups=mesh['ctx'=16,'tp'=4,'dp'=4] {'tp'}, dimensions={0} | all-to-all | bytes 1049600 | tf_op jit(solution)/shard_map/all_to_all | solution.py:41
  137.5 10.5 %all_to_all.37 = bf16[4,64,1024]{2,1,0:T(8,128)(2,1)S(1)} all-to-all(bf16[4,64,1024]{2,1,0:T(8,128)(2,1)S(1)} %broadcast_in_dim.42), channel_id=1, replica_groups=mesh['ctx'=16,'tp'=4,'dp'=4] {'tp'}, dimensions={0} | all-to-all | bytes 1048576 | tf_op jit(solution)/shard_map/all_to_all | solution.py:27
  148.0 2.3 convolution_convert_fusion.3
  151.3 25.1 %all_to_all.38 = bf16[4,256,1024]{1,2,0:T(8,128)(2,1)S(1)} all-to-all(bf16[4,256,1024]{1,2,0:T(8,128)(2,1)S(1)} %broadcast_in_dim.43), channel_id=1, replica_groups=mesh['ctx'=16,'tp'=4,'dp'=4] {'tp'}, dimensions={0} | all-to-all | bytes 4194304 | tf_op jit(solution)/shard_map/all_to_all | solution.py:27
  177.0 1.7 fusion.14
  178.7 45.8 %all-gather.7.cloned.1.call-done = bf16[4096,768]{1,0:T(8,128)(2,1)} async-done(((bf16[256,768]{1,0:T(8,128)(2,1)}), bf16[4096,768]{1,0:T(8,128)(2,1)}) %all-gather.7.cloned.1.call-update) | async-done | bytes 6291472 | tf_op jit(solution)/shard_map/all_gather | solution.py:62
  224.5 2.4 convolution_convert_fusion.4
  226.9 2.4 convolution_convert_fusion.5
  232.1 4.4 compare_select_fusion.1
  236.5 5.5 %fusion.63 = pred[4096]{0:T(1024)(128)(4,1)S(1)} fusion(pred[4096]{0:T(1024)(128)(4,1)S(1)} %compare_reduce_fusion, pred[4096]{0:T(1024)(128)(4,1)S(1)} %compare_reduce_fusion.1, pred[4096]{0:T(1024)(128)(4,1)S(1)} %compare_reduce_fusion.2, pred[4096]{0:T(1024)(128)(4,1)S(1)} %compare_reduce_fusion.3, pred[4096]{0:T(1024)(128)(4,1)S(1)} %compare_reduce_fusion.4, ...), kind=kLoop, calls=%fused_computation.96 | loop fusion | flops 65536 | bytes 57380 | tf_op jit(solution)/shard_map/lt | solution.py:199
  242.0 3.4 fusion.27
  245.6 62.1 %all-gather.9.cloned.1.call-done = bf16[4096,256]{0,1:T(8,128)(2,1)} async-done(((bf16[256,256]{0,1:T(8,128)(2,1)}), bf16[4096,256]{0,1:T(8,128)(2,1)}) %all-gather.9.cloned.1.call-update) | async-done | bytes 2097168 | tf_op jit(solution)/shard_map/all_gather | solution.py:62
  307.7 6.7 %fusion.2 = (f32[1024]{0:T(1024)S(1)}, f32[1024,4096]{1,0:T(8,128)S(1)}) fusion(s32[1024]{0:T(1024)S(1)} %bitcast.109, pred[4096]{0:T(1024)(128)(4,1)S(1)} %fusion.63, bf16[1024,128]{1,0:T(8,128)(2,1)S(1)} %bitcast.106, bf16[4096,256]{0,1:T(8,128)(2,1)} %all-gather.9.cloned.1.call-done), kind=kOutput, calls=%fused_computation.5 | convolution fusion | flops 1094712320 | bytes 18100224 | tf_op jit(solution)/shard_map/hqd,hkd->hqk/dot_general | solution.py:202
  314.4 7.7 %fusion.70 = f32[1024]{0:T(1024)S(1)} fusion(f32[1024]{0:T(1024)S(1)} %broadcast_maximum_fusion, f32[1024,4096]{1,0:T(8,128)S(1)} %get-tuple-element.32, s32[1024]{0:T(1024)S(1)} %bitcast.110, pred[4096]{0:T(1024)(128)(4,1)S(1)} %fusion.63), kind=kLoop, calls=%fused_computation.123 | loop fusion | flops 29359104 | bytes 16793600 | tf_op jit(solution)/shard_map/reduce_sum | solution.py:207
  322.1 6.0 %fusion.24 = bf16[1024,128]{1,0:T(8,128)(2,1)S(1)} fusion(bf16[4096,256]{0,1:T(8,128)(2,1)S(1)} %copy-done.11, f32[1024]{0:T(1024)S(1)} %fusion.70, f32[1024,4096]{1,0:T(8,128)S(1)} %get-tuple-element.32, f32[1024]{0:T(1024)S(1)} %broadcast_maximum_fusion, s32[1024]{0:T(1024)S(1)} %bitcast.111, pred[4096]{0:T(1024)(128)(4,1)S(1)} %fusion.63), kind=kOutput, calls=%fused_computation.37 | convolution fusion | flops 1103364096 | bytes 18104320 | tf_op jit(solution)/shard_map/hqk,hkd->hqd/dot_general | solution.py:208
  328.3 61.0 %all-gather.11.cloned.1.call-done = bf16[512,4096]{1,0:T(8,128)(2,1)} async-done(((bf16[512,256]{1,0:T(8,128)(2,1)}), bf16[512,4096]{1,0:T(8,128)(2,1)}) %all-gather.11.cloned.1.call-update) | async-done | bytes 4194320 | tf_op jit(solution)/shard_map/all_gather | solution.py:220
  389.2 3.5 convolution_convert_fusion
  392.9 27.9 %all_to_all.39 = bf16[4,256,1024]{2,1,0:T(8,128)(2,1)} all-to-all(bf16[4,256,1024]{2,1,0:T(8,128)(2,1)S(1)} %bitcast.97), channel_id=1, replica_groups=mesh['ctx'=16,'tp'=4,'dp'=4] {'tp'}, dimensions={0} | all-to-all | bytes 4194304 | tf_op jit(solution)/shard_map/all_to_all | solution.py:41
  420.8 1.6 stack.2
  422.4 9.0 %all-to-all-start.5 = ((bf16[16,1024,64]{1,2,0:T(8,128)(2,1)}), bf16[16,1024,64]{1,2,0:T(8,128)(2,1)S(1)}, u32[]{:S(2)}, u32[]{:S(2)}) async-start(bf16[16,1024,64]{1,2,0:T(8,128)(2,1)} %stack.2), calls=%async_computation.5 | async-start | bytes 4194304 | tf_op jit(solution)/shard_map/all_to_all | solution.py:226
  431.5 2.1 convert_reduce_fusion
  433.5 46.2 %all-to-all-done.5 = bf16[16,1024,64]{1,2,0:T(8,128)(2,1)S(1)} async-done(((bf16[16,1024,64]{1,2,0:T(8,128)(2,1)}), bf16[16,1024,64]{1,2,0:T(8,128)(2,1)S(1)}, u32[]{:S(2)}, u32[]{:S(2)}) %all-to-all-start.5) | async-done | bytes 2097184 | tf_op jit(solution)/shard_map/all_to_all | solution.py:226
  479.8 1.8 convolution_convert_fusion.2
  483.2 4.4 all-to-all-start.6
  487.6 25.8 %all-to-all-done.6 = bf16[4,256,1024]{2,1,0:T(8,128)(2,1)} async-done(((bf16[4,256,1024]{2,1,0:T(8,128)(2,1)}), bf16[4,256,1024]{2,1,0:T(8,128)(2,1)}, u32[]{:S(2)}, u32[]{:S(2)}) %all-to-all-start.6) | async-done | bytes 2097184 | tf_op jit(solution)/shard_map/all_to_all | solution.py:27
  513.4 2.0 reduce_sum.115
  515.4 2.5 collective-permute-start.6
  517.9 8.1 %collective-permute-done.6 = bf16[1,1024]{1,0:T(2,128)(2,1)S(1)} collective-permute-done((bf16[1,1024]{1,0:T(2,128)(2,1)S(1)}, bf16[1,1024]{1,0:T(2,128)(2,1)S(1)}, u32[]{:S(2)}, u32[]{:S(2)}) %collective-permute-start.6) | collective-permute-done | bytes 2080 | tf_op jit(solution)/shard_map/ppermute | solution.py:16
  (100 shorter events, 20.4 us)
Async XLA Ops:
  6.5 112.9 %copy-start = (bf16[1024,1024]{1,0:T(8,128)(2,1)S(1)}, bf16[1024,1024]{1,0:T(8,128)(2,1)}, u32[]{:S(2)}) copy-start(bf16[1024,1024]{1,0:T(8,128)(2,1)} %param.16) | copy-start | bytes 6291460
  6.5 141.5 %all-gather.5.cloned.1.call-start = ((), (), s32[]{:S(2)}) async-start(), calls=%async_computation.7 | async-start | bytes 2228224 | tf_op jit(solution)/shard_map/all_gather | solution.py:171
  7.3 217.2 %all-gather.7.cloned.1.call-start = ((), (), s32[]{:S(2)}) async-start(), calls=%async_computation.8 | async-start | bytes 6684672 | tf_op jit(solution)/shard_map/all_gather | solution.py:62
  11.8 37.8 %all-to-all-start = ((s32[64,1,1]{2,1,0:T(1,128)}), s32[64,1,1]{2,1,0:T(1,128)S(1)}, u32[]{:S(2)}, u32[]{:S(2)}) async-start(s32[64,1,1]{2,1,0:T(1,128)} %broadcast_in_dim.40), calls=%async_computation | async-start | bytes 65536 | tf_op jit(solution)/shard_map/all_to_all | solution.py:27
  25.5 282.2 %all-gather.9.cloned.1.call-start = ((), (), s32[]{:S(2)}) async-start(), calls=%async_computation.9 | async-start | bytes 2228224 | tf_op jit(solution)/shard_map/all_gather | solution.py:62
  26.8 12.5 %copy-start.10 = (s32[256]{0:T(256)S(1)}, s32[256]{0:T(256)}, u32[]{:S(2)}) copy-start(s32[256]{0:T(256)} %param.13) | copy-start | bytes 3076
  32.6 22.6 %collective-permute-start = (bf16[256,1024]{1,0:T(8,128)(2,1)}, bf16[256,1024]{1,0:T(8,128)(2,1)}, u32[]{:S(2)}, u32[]{:S(2)}) collective-permute-start(bf16[256,1024]{1,0:T(8,128)(2,1)} %get-tuple-element.8), channel_id=1, source_target_pairs={{0,4},{4,8},{8,12},{12,16},{16,20},{20,24},{24,28},{28,32},{32,36}... | collective-permute-start | bytes 1572872 | tf_op jit(solution)/shard_map/ppermute | solution.py:16
  36.0 43.4 %collective-permute-start.2 = (bf16[256,1024]{1,0:T(8,128)(2,1)S(1)}, bf16[256,1024]{1,0:T(8,128)(2,1)}, u32[]{:S(2)}, u32[]{:S(2)}) collective-permute-start(bf16[256,1024]{1,0:T(8,128)(2,1)S(1)} %get-tuple-element.9), channel_id=1, source_target_pairs={{0,4},{4,8},{8,12},{12,16},{16,20},{20,24},{24,28},{28,32},{32,36}... | collective-permute-start | bytes 1572872 | tf_op jit(solution)/shard_map/ppermute | solution.py:16
  40.6 41.6 %collective-permute-start.5 = (f32[1]{0:T(128)}, f32[1]{0:T(128)}, u32[]{:S(2)}, u32[]{:S(2)}) collective-permute-start(f32[1]{0:T(128)} %bitcast.15), channel_id=1, source_target_pairs={{4,0},{8,4},{12,8},{16,12},{20,16},{24,20},{28,24},{32,28},{36,32}... | collective-permute-start | bytes 20 | tf_op jit(solution)/shard_map/ppermute | solution.py:16
  55.2 35.3 %collective-permute-start.1 = (bf16[256,1024]{1,0:T(8,128)(2,1)}, bf16[256,1024]{1,0:T(8,128)(2,1)S(1)}, u32[]{:S(2)}, u32[]{:S(2)}) collective-permute-start(bf16[256,1024]{1,0:T(8,128)(2,1)} %collective-permute-done), channel_id=1, source_target_pairs={{0,4},{4,8},{8,12},{12,16},{16,20},{20,24},{24,28},{28,32},{32,36}... | collective-permute-start | bytes 1572872 | tf_op jit(solution)/shard_map/ppermute | solution.py:16
  79.4 21.2 %collective-permute-start.3 = (bf16[256,1024]{1,0:T(8,128)(2,1)}, bf16[256,1024]{1,0:T(8,128)(2,1)}, u32[]{:S(2)}, u32[]{:S(2)}) collective-permute-start(bf16[256,1024]{1,0:T(8,128)(2,1)} %collective-permute-done.2), channel_id=1, source_target_pairs={{0,4},{4,8},{8,12},{12,16},{16,20},{20,24},{24,28},{28,32},{32,36}... | collective-permute-start | bytes 1572872 | tf_op jit(solution)/shard_map/ppermute | solution.py:16
  93.0 12.7 %copy-start.7 = (bf16[256,1024]{0,1:T(8,128)(2,1)S(1)}, bf16[256,1024]{0,1:T(8,128)(2,1)}, u32[]{:S(2)}) copy-start(bf16[256,1024]{0,1:T(8,128)(2,1)} %copy.46) | copy-start | bytes 1572868
  114.1 5.3 copy-start.3
  120.2 30.2 %copy-start.4 = (bf16[256,1024]{1,0:T(8,128)(2,1)}, bf16[256,1024]{1,0:T(8,128)(2,1)S(1)}, u32[]{:S(2)}) copy-start(bf16[256,1024]{1,0:T(8,128)(2,1)S(1)} %fusion.18) | copy-start | bytes 1572868
  120.3 5.5 %collective-permute-start.4 = (f32[1,1024]{1,0:T(1,128)S(1)}, f32[1,1024]{1,0:T(1,128)S(1)}, u32[]{:S(2)}, u32[]{:S(2)}) collective-permute-start(f32[1,1024]{1,0:T(1,128)S(1)} %fusion.76), channel_id=1, source_target_pairs={{4,0},{8,4},{12,8},{16,12},{20,16},{24,20},{28,24},{32,28},{36,32}... | collective-permute-start | bytes 12296 | tf_op jit(solution)/shard_map/ppermute | solution.py:16
  150.3 0.8 copy-start.6
  151.2 25.8 %copy-start.9 = (f32[4096]{0:T(1024)S(1)}, f32[4096]{0:T(1024)}, u32[]{:S(2)}) copy-start(f32[4096]{0:T(1024)} %param.18) | copy-start | bytes 49156
  178.7 63.3 %copy-start.2 = (bf16[256,4096]{0,1:T(8,128)(2,1)S(1)}, bf16[256,4096]{0,1:T(8,128)(2,1)}, u32[]{:S(2)}) copy-start(bf16[256,4096]{0,1:T(8,128)(2,1)} %fusion.14) | copy-start | bytes 6291460
  230.0 159.2 %all-gather.11.cloned.1.call-start = ((), (), s32[]{:S(2)}) async-start(), calls=%async_computation.10 | async-start | bytes 4456448 | tf_op jit(solution)/shard_map/all_gather | solution.py:220
  314.4 7.7 %copy-start.11 = (bf16[4096,256]{0,1:T(8,128)(2,1)S(1)}, bf16[4096,256]{0,1:T(8,128)(2,1)}, u32[]{:S(2)}) copy-start(bf16[4096,256]{0,1:T(8,128)(2,1)} %all-gather.9.cloned.1.call-done) | copy-start | bytes 6291460
  392.7 28.1 %copy-start.8 = (bf16[1024,64]{0,1:T(8,128)(2,1)S(1)}, bf16[1024,64]{0,1:T(8,128)(2,1)}, u32[]{:S(2)}) copy-start(bf16[1024,64]{0,1:T(8,128)(2,1)} %param.23) | copy-start | bytes 393220
  422.4 57.3 %all-to-all-start.5 = ((bf16[16,1024,64]{1,2,0:T(8,128)(2,1)}), bf16[16,1024,64]{1,2,0:T(8,128)(2,1)S(1)}, u32[]{:S(2)}, u32[]{:S(2)}) async-start(bf16[16,1024,64]{1,2,0:T(8,128)(2,1)} %stack.2), calls=%async_computation.5 | async-start | bytes 4194304 | tf_op jit(solution)/shard_map/all_to_all | solution.py:226
  481.6 44.5 %copy-start.5 = (bf16[256,1024]{1,0:T(8,128)(2,1)S(1)}, bf16[256,1024]{1,0:T(8,128)(2,1)}, u32[]{:S(2)}) copy-start(bf16[256,1024]{1,0:T(8,128)(2,1)} %copy-done.4) | copy-start | bytes 1572868
  481.6 45.7 %copy-start.1 = (bf16[1024,1024]{1,0:T(8,128)(2,1)S(1)}, bf16[1024,1024]{1,0:T(8,128)(2,1)}, u32[]{:S(2)}) copy-start(bf16[1024,1024]{1,0:T(8,128)(2,1)} %param.16) | copy-start | bytes 6291460
  483.2 30.2 %all-to-all-start.6 = ((bf16[4,256,1024]{2,1,0:T(8,128)(2,1)}), bf16[4,256,1024]{2,1,0:T(8,128)(2,1)}, u32[]{:S(2)}, u32[]{:S(2)}) async-start(bf16[4,256,1024]{2,1,0:T(8,128)(2,1)} %broadcast_in_dim.82), calls=%async_computation.6 | async-start | bytes 4194304 | tf_op jit(solution)/shard_map/all_to_all | solution.py:27
  515.4 10.6 %collective-permute-start.6 = (bf16[1,1024]{1,0:T(2,128)(2,1)S(1)}, bf16[1,1024]{1,0:T(2,128)(2,1)S(1)}, u32[]{:S(2)}, u32[]{:S(2)}) collective-permute-start(bf16[1,1024]{1,0:T(2,128)(2,1)S(1)} %constant_dynamic-slice_fusion), channel_id=1, source_target_pairs={{0,4},{4,8},{8,12},{12,16},{16,20},{20,24},{24,28},{28,32},{32,36}... | collective-permute-start | bytes 6152 | tf_op jit(solution)/shard_map/ppermute | solution.py:16
Sparse Core Ops, SparseCore 0:
  9.8 61.1 all-gather.4
  73.4 151.0 all-gather.6
  230.1 77.5 all-gather.8
  310.0 79.2 all-gather.10
